TPU v7x, 32 devices: a whole 2x2x4 slice. The times are simulated.
32 devices in a mesh: ep: 4 (over y, core), fs: 8 (over z, x).
Axes of the slice: x: 2, y: 2, z: 4, core: 2. Of those that a mesh axis runs over, the one named last changes fastest.
Arguments:
- grads: bfloat16 [4, 4, 128, 14336], P('ep', None, 'fs'), may hold values from -64 to 64
- counts: int32 [4, 4], replicated, may hold values from 16 to 2047
- weight: bfloat16 [4, 128, 14336], P('ep', 'fs'), may hold values from -3 to 3
- mom: float32 [4, 128, 14336], P('ep', 'fs'), may hold values from -64 to 64
- second: float32 [4, 128, 14336], P('ep', 'fs'), may hold values from 0.1 to 10
- in_weight: float32 [6, 32], replicated, may hold values from -2.5 to 2.5
- in_bias: float32 [32], replicated, may hold values from -3 to 3
- out_weight: float32 [32, 2], replicated, may hold values from -1 to 1
- out_bias: float32 [2], replicated, may hold values from -3 to 3
Outputs:
- new_weight: bfloat16 [4, 128, 14336], P('ep')
- new_mom: float32 [4, 128, 14336], P('ep', 'fs')
- new_second: float32 [4, 128, 14336], P('ep', 'fs')
All inputs are finite; a program needn't handle non-finite values.
Results may differ from a plain program's by a relative error of at most 0.0019.
Values may be sent and summed in bfloat16 or wider, within the bound.
A program may use at most 64 MiB of HBM per device.

v0:
```python
import jax
import jax.numpy as jnp
from jax import lax
from jax.sharding import PartitionSpec as P

MOMENTUM_DECAY = 0.9
SECOND_DECAY = 0.99
NORM_EPS = 1e-06
ROOT_EPS = 1e-08
STEP_SCALE = 0.2
EXP_SCALE = 0.5


def learned_step(
    gradient,
    mom_next,
    second_next,
    weight,
    grad_norm,
    mom_norm,
    in_weight,
    in_bias,
    out_weight,
    out_bias,
):
    inv_root = lax.rsqrt(second_next + ROOT_EPS)
    features = jnp.stack(
        [
            gradient / grad_norm,
            mom_next / mom_norm,
            mom_next * inv_root,
            gradient * inv_root,
            weight.astype(jnp.float32),
            jnp.broadcast_to(jnp.log(mom_norm), gradient.shape),
        ]
    )
    hidden = jax.nn.relu(
        jnp.einsum("fh,fab->hab", in_weight, features, precision=lax.Precision.HIGHEST)
        + in_bias[:, None, None]
    )
    outputs = (
        jnp.einsum("hk,hab->kab", out_weight, hidden, precision=lax.Precision.HIGHEST)
        + out_bias[:, None, None]
    )
    update = STEP_SCALE * outputs[0] * jnp.exp(EXP_SCALE * outputs[1])
    return (weight.astype(jnp.float32) - update).astype(jnp.bfloat16)


def add_sources(arrived):
    return jnp.sum(arrived.astype(jnp.float32), axis=0)


def per_device(grads, counts, weight, mom, second, in_weight, in_bias, out_weight, out_bias):
    source = lax.axis_index("ep")
    counts_f = counts.astype(jnp.float32)
    totals = jnp.sum(counts_f, axis=0)
    share_row = lax.dynamic_index_in_dim(counts_f, source, 0, keepdims=False) / totals
    weighted = share_row[None, :, None, None] * grads.astype(jnp.float32)
    outgoing = weighted.astype(jnp.bfloat16)
    gradient = add_sources(lax.all_to_all(outgoing, "ep", split_axis=1, concat_axis=0, tiled=True))[
        0
    ]
    mom_here = mom[0]
    second_here = second[0]
    mom_next = MOMENTUM_DECAY * mom_here + (1.0 - MOMENTUM_DECAY) * gradient
    second_next = SECOND_DECAY * second_here + (1.0 - SECOND_DECAY) * gradient * gradient
    entries = gradient.shape[0] * gradient.shape[1] * lax.axis_size("fs")
    grad_sq, mom_sq = lax.psum((jnp.sum(gradient * gradient), jnp.sum(mom_next * mom_next)), "fs")
    grad_norm = jnp.sqrt(grad_sq / entries + NORM_EPS)
    mom_norm = jnp.sqrt(mom_sq / entries + NORM_EPS)
    width = gradient.shape[1]

    def block_step(items):
        grad_block, mom_block, second_block, weight_block = items
        return learned_step(
            grad_block,
            mom_block,
            second_block,
            weight_block,
            grad_norm,
            mom_norm,
            in_weight,
            in_bias,
            out_weight,
            out_bias,
        )

    blocks = lax.map(
        block_step,
        (
            gradient.reshape(-1, 2, width),
            mom_next.reshape(-1, 2, width),
            second_next.reshape(-1, 2, width),
            weight[0].reshape(-1, 2, width),
        ),
    )
    updated = blocks.reshape(gradient.shape)
    gathered = lax.all_gather(updated[None], "fs", axis=1, tiled=True)
    return (gathered, mom_next[None], second_next[None])


def solution(mesh):
    in_specs = (
        P("ep", None, "fs", None),
        P(),
        P("ep", "fs", None),
        P("ep", "fs", None),
        P("ep", "fs", None),
        P(),
        P(),
        P(),
        P(),
    )
    out_specs = (P("ep", None, None), P("ep", "fs", None), P("ep", "fs", None))
    return jax.shard_map(
        per_device, mesh=mesh, in_specs=in_specs, out_specs=out_specs, check_vma=False
    )
```

profile of v0, /device:TPU:0, one launch (start us, length us, event | category | flops | bytes accessed | tf_op | source)
XLA Modules:
  0.0 230.4 jit_solution(16413111683950979025)
XLA Ops:
  8.6 3.1 %multiply_convert_fusion = bf16[1,4,16,14336]{3,2,0,1:T(8,128)(2,1)} fusion(bf16[1,4,16,14336]{3,2,1,0:T(8,128)(2,1)} %param.11, f32[4]{0:T(128)S(1)} %bitcast_divide_fusion), kind=kLoop, calls=%fused_computation.22 | loop fusion | flops 2752512 | bytes 3670032 | tf_op jit(solution)/shard_map/convert_element_type | solution.py:59
  11.7 4.3 %all-to-all-start = ((bf16[1,4,16,14336]{3,2,0,1:T(8,128)(2,1)}), bf16[1,4,16,14336]{3,2,0,1:T(8,128)(2,1)S(1)}, u32[]{:S(2)}, u32[]{:S(2)}) async-start(bf16[1,4,16,14336]{3,2,0,1:T(8,128)(2,1)} %multiply_convert_fusion), calls=%async_computation | async-start | bytes 3670016 | tf_op jit(solution)/shard_map/all_to_all | solution.py:60
  16.3 22.5 %all-to-all-done = bf16[1,4,16,14336]{3,2,0,1:T(8,128)(2,1)S(1)} async-done(((bf16[1,4,16,14336]{3,2,0,1:T(8,128)(2,1)}), bf16[1,4,16,14336]{3,2,0,1:T(8,128)(2,1)S(1)}, u32[]{:S(2)}, u32[]{:S(2)}) %all-to-all-start) | async-done | bytes 1835040 | tf_op jit(solution)/shard_map/all_to_all | solution.py:60
  42.6 23.1 %all-reduce = (f32[]{:T(128)}, f32[]{:T(128)}) all-reduce(f32[]{:T(128)} %get-tuple-element.159, f32[]{:T(128)} %get-tuple-element.158), channel_id=1, replica_groups=mesh['ep'=4,'fs'=8] {'fs'}, use_global_device_ids=true, to_apply=%region_3.4 | all-reduce | flops 2 | bytes 16 | tf_op jit(solution)/shard_map/psum | solution.py:68
  66.5 3.0 %fusion.10 = (f32[1,16,14336]{2,1,0:T(8,128)}, f32[1,16,14336]{2,1,0:T(8,128)S(1)}, f32[1,16,14336]{2,1,0:T(8,128)}, f32[1,16,14336]{2,1,0:T(8,128)S(1)}) fusion(f32[16,14336]{1,0:T(8,128)S(1)} %convert_reduce_fusion, f32[1,16,14336]{2,1,0:T(8,128)} %param.15, f32[1,16,14336]{2,1,0:T(8,128)} %param.14), kind=kLoop, calls=%fused_computation.26 | loop fusion | flops 1605632 | bytes 6422528 | tf_op jit(solution)/shard_map/add | solution.py:66
  72.2 4.1 %fusion.9 = (f32[8,2,14336]{2,0,1:T(8,128)S(1)}, f32[8,2,14336]{2,0,1:T(8,128)}, f32[8,2,14336]{2,0,1:T(8,128)}) fusion(f32[8,2,14336]{2,1,0:T(2,128)S(1)} %mul.131, f32[8,2,14336]{2,1,0:T(2,128)S(1)} %copy-done, f32[8,2,14336]{2,1,0:T(2,128)} %mul.122), kind=kLoop, calls=%fused_computation.25 | loop fusion | flops 1146880 | bytes 5505024 | tf_op jit(solution)/shard_map/add | solution.py:66
  76.3 78.5 %while.11 = (s32[]{:T(128)}, bf16[8,2,14336]{2,1,0:T(2,128)(2,1)}, bf16[8,2,14336]{2,1,0:T(2,128)(2,1)S(1)}, f32[8,2,14336]{2,0,1:T(8,128)}, f32[]{:T(128)}, /*i...) while((s32[]{:T(128)}, bf16[8,2,14336]{2,1,0:T(2,128)(2,1)}, ...), condition=%wide.region_7.8_spmd, body=%wide.region_6.7_spmd.sunk | while | flops 90316800 | bytes 18638680 | solution.py:88
  76.3 2.2 dynamic-slice_multiply_fusion.3
  79.9 3.2 %fusion.27 = f32[32,2,14336]{2,0,1:T(8,128)S(1)} fusion(f32[6,2,14336]{2,0,1:T(8,128)S(1)} %stack.4, f32[32]{0:T(128)S(1)} %get-tuple-element.324, f32[6,32]{1,0:T(8,128)S(1)} %get-tuple-element.323), kind=kOutput, calls=%fused_computation.2.clone.1 | convolution fusion | flops 67895296 | bytes 4359040 | tf_op jit(solution)/shard_map/while/body/eval_jaxpr/fh,fab->hab/dot_general | solution.py:38
  86.2 2.2 dynamic-slice_multiply_fusion.3
  89.7 3.2 %fusion.27 = f32[32,2,14336]{2,0,1:T(8,128)S(1)} fusion(f32[6,2,14336]{2,0,1:T(8,128)S(1)} %stack.4, f32[32]{0:T(128)S(1)} %get-tuple-element.324, f32[6,32]{1,0:T(8,128)S(1)} %get-tuple-element.323), kind=kOutput, calls=%fused_computation.2.clone.1 | convolution fusion | flops 67895296 | bytes 4359040 | tf_op jit(solution)/shard_map/while/body/eval_jaxpr/fh,fab->hab/dot_general | solution.py:38
  96.0 2.2 dynamic-slice_multiply_fusion.3
  99.5 3.2 %fusion.27 = f32[32,2,14336]{2,0,1:T(8,128)S(1)} fusion(f32[6,2,14336]{2,0,1:T(8,128)S(1)} %stack.4, f32[32]{0:T(128)S(1)} %get-tuple-element.324, f32[6,32]{1,0:T(8,128)S(1)} %get-tuple-element.323), kind=kOutput, calls=%fused_computation.2.clone.1 | convolution fusion | flops 67895296 | bytes 4359040 | tf_op jit(solution)/shard_map/while/body/eval_jaxpr/fh,fab->hab/dot_general | solution.py:38
  105.8 2.2 dynamic-slice_multiply_fusion.3
  109.3 3.2 %fusion.27 = f32[32,2,14336]{2,0,1:T(8,128)S(1)} fusion(f32[6,2,14336]{2,0,1:T(8,128)S(1)} %stack.4, f32[32]{0:T(128)S(1)} %get-tuple-element.324, f32[6,32]{1,0:T(8,128)S(1)} %get-tuple-element.323), kind=kOutput, calls=%fused_computation.2.clone.1 | convolution fusion | flops 67895296 | bytes 4359040 | tf_op jit(solution)/shard_map/while/body/eval_jaxpr/fh,fab->hab/dot_general | solution.py:38
  115.6 2.2 dynamic-slice_multiply_fusion.3
  119.1 3.2 %fusion.27 = f32[32,2,14336]{2,0,1:T(8,128)S(1)} fusion(f32[6,2,14336]{2,0,1:T(8,128)S(1)} %stack.4, f32[32]{0:T(128)S(1)} %get-tuple-element.324, f32[6,32]{1,0:T(8,128)S(1)} %get-tuple-element.323), kind=kOutput, calls=%fused_computation.2.clone.1 | convolution fusion | flops 67895296 | bytes 4359040 | tf_op jit(solution)/shard_map/while/body/eval_jaxpr/fh,fab->hab/dot_general | solution.py:38
  128.9 3.2 %fusion.27 = f32[32,2,14336]{2,0,1:T(8,128)S(1)} fusion(f32[6,2,14336]{2,0,1:T(8,128)S(1)} %stack.4, f32[32]{0:T(128)S(1)} %get-tuple-element.324, f32[6,32]{1,0:T(8,128)S(1)} %get-tuple-element.323), kind=kOutput, calls=%fused_computation.2.clone.1 | convolution fusion | flops 67895296 | bytes 4359040 | tf_op jit(solution)/shard_map/while/body/eval_jaxpr/fh,fab->hab/dot_general | solution.py:38
  135.2 2.2 dynamic-slice_multiply_fusion.3
  138.7 3.2 %fusion.27 = f32[32,2,14336]{2,0,1:T(8,128)S(1)} fusion(f32[6,2,14336]{2,0,1:T(8,128)S(1)} %stack.4, f32[32]{0:T(128)S(1)} %get-tuple-element.324, f32[6,32]{1,0:T(8,128)S(1)} %get-tuple-element.323), kind=kOutput, calls=%fused_computation.2.clone.1 | convolution fusion | flops 67895296 | bytes 4359040 | tf_op jit(solution)/shard_map/while/body/eval_jaxpr/fh,fab->hab/dot_general | solution.py:38
  145.0 2.2 dynamic-slice_multiply_fusion.3
  148.5 3.2 %fusion.27 = f32[32,2,14336]{2,0,1:T(8,128)S(1)} fusion(f32[6,2,14336]{2,0,1:T(8,128)S(1)} %stack.4, f32[32]{0:T(128)S(1)} %get-tuple-element.324, f32[6,32]{1,0:T(8,128)S(1)} %get-tuple-element.323), kind=kOutput, calls=%fused_computation.2.clone.1 | convolution fusion | flops 67895296 | bytes 4359040 | tf_op jit(solution)/shard_map/while/body/eval_jaxpr/fh,fab->hab/dot_general | solution.py:38
  156.8 62.5 %all-gather.2.cloned.1.call-done = bf16[1,128,14336]{2,1,0:T(8,128)(2,1)} async-done(((bf16[1,16,14336]{2,1,0:T(8,128)(2,1)}), bf16[1,128,14336]{2,1,0:T(8,128)(2,1)}) %all-gather.2.cloned.1.call-update) | async-done | bytes 3670032 | tf_op jit(solution)/shard_map/all_gather | solution.py:98
  219.3 4.2 %copy.64 = bf16[1,128,14336]{2,1,0:T(8,128)(2,1)} copy(bf16[1,128,14336]{2,1,0:T(8,128)(2,1)} %all-gather.2.cloned.1.call-done) | data formatting | bytes 7340032
  (114 shorter events, 46.7 us)
Async XLA Ops:
  8.6 7.4 %copy-start.3 = (bf16[1,16,14336]{2,1,0:T(8,128)(2,1)S(1)}, bf16[1,16,14336]{2,1,0:T(8,128)(2,1)}, u32[]{:S(2)}) copy-start(bf16[1,16,14336]{2,1,0:T(8,128)(2,1)} %param.13) | copy-start | bytes 1376260
  11.7 27.1 %all-to-all-start = ((bf16[1,4,16,14336]{3,2,0,1:T(8,128)(2,1)}), bf16[1,4,16,14336]{3,2,0,1:T(8,128)(2,1)S(1)}, u32[]{:S(2)}, u32[]{:S(2)}) async-start(bf16[1,4,16,14336]{3,2,0,1:T(8,128)(2,1)} %multiply_convert_fusion), calls=%async_computation | async-start | bytes 3670016 | tf_op jit(solution)/shard_map/all_to_all | solution.py:60
  16.0 203.3 %all-gather.2.cloned.1.call-start = ((), (), s32[]{:S(2)}) async-start(), calls=%async_computation.1 | async-start | bytes 4128768 | tf_op jit(solution)/shard_map/all_gather | solution.py:98
  69.4 2.8 %copy-start = (f32[8,2,14336]{2,1,0:T(2,128)S(1)}, f32[8,2,14336]{2,1,0:T(2,128)}, u32[]{:S(2)}) copy-start(f32[8,2,14336]{2,1,0:T(2,128)} %reshape_squeeze.7) | copy-start | bytes 2752516
  70.9 5.4 %copy-start.4 = (f32[6,32]{1,0:T(8,128)S(1)}, f32[6,32]{1,0:T(8,128)}, u32[]{:S(2)}) copy-start(f32[6,32]{1,0:T(8,128)} %param.16) | copy-start | bytes 2308
  70.9 5.4 %copy-start.5 = (f32[32,2]{0,1:T(2,128)S(1)}, f32[32,2]{0,1:T(2,128)}, u32[]{:S(2)}) copy-start(f32[32,2]{0,1:T(2,128)} %param.18) | copy-start | bytes 772
  70.9 5.4 %copy-start.6 = (f32[32]{0:T(128)S(1)}, f32[32]{0:T(128)}, u32[]{:S(2)}) copy-start(f32[32]{0:T(128)} %param.17) | copy-start | bytes 388
  70.9 5.4 %copy-start.7 = (f32[2]{0:T(128)S(1)}, f32[2]{0:T(128)}, u32[]{:S(2)}) copy-start(f32[2]{0:T(128)} %param.19) | copy-start | bytes 28
  76.3 2.2 copy-start.1
  83.1 3.1 %copy-start.2 = (f32[8,2,14336]{2,0,1:T(8,128)S(1)}, f32[8,2,14336]{2,0,1:T(8,128)}, u32[]{:S(2)}) copy-start(f32[8,2,14336]{2,0,1:T(8,128)} %copy-done.1) | copy-start | bytes 2752516 | tf_op jit(solution)/shard_map/while
  86.2 2.2 copy-start.1
  92.9 3.1 %copy-start.2 = (f32[8,2,14336]{2,0,1:T(8,128)S(1)}, f32[8,2,14336]{2,0,1:T(8,128)}, u32[]{:S(2)}) copy-start(f32[8,2,14336]{2,0,1:T(8,128)} %copy-done.1) | copy-start | bytes 2752516 | tf_op jit(solution)/shard_map/while
  96.0 2.2 copy-start.1
  102.7 3.1 %copy-start.2 = (f32[8,2,14336]{2,0,1:T(8,128)S(1)}, f32[8,2,14336]{2,0,1:T(8,128)}, u32[]{:S(2)}) copy-start(f32[8,2,14336]{2,0,1:T(8,128)} %copy-done.1) | copy-start | bytes 2752516 | tf_op jit(solution)/shard_map/while
  105.8 2.2 copy-start.1
  112.5 3.1 %copy-start.2 = (f32[8,2,14336]{2,0,1:T(8,128)S(1)}, f32[8,2,14336]{2,0,1:T(8,128)}, u32[]{:S(2)}) copy-start(f32[8,2,14336]{2,0,1:T(8,128)} %copy-done.1) | copy-start | bytes 2752516 | tf_op jit(solution)/shard_map/while
  115.6 2.2 copy-start.1
  122.3 3.1 %copy-start.2 = (f32[8,2,14336]{2,0,1:T(8,128)S(1)}, f32[8,2,14336]{2,0,1:T(8,128)}, u32[]{:S(2)}) copy-start(f32[8,2,14336]{2,0,1:T(8,128)} %copy-done.1) | copy-start | bytes 2752516 | tf_op jit(solution)/shard_map/while
  125.4 2.2 copy-start.1
  132.1 3.1 %copy-start.2 = (f32[8,2,14336]{2,0,1:T(8,128)S(1)}, f32[8,2,14336]{2,0,1:T(8,128)}, u32[]{:S(2)}) copy-start(f32[8,2,14336]{2,0,1:T(8,128)} %copy-done.1) | copy-start | bytes 2752516 | tf_op jit(solution)/shard_map/while
  135.2 2.2 copy-start.1
  141.9 3.1 %copy-start.2 = (f32[8,2,14336]{2,0,1:T(8,128)S(1)}, f32[8,2,14336]{2,0,1:T(8,128)}, u32[]{:S(2)}) copy-start(f32[8,2,14336]{2,0,1:T(8,128)} %copy-done.1) | copy-start | bytes 2752516 | tf_op jit(solution)/shard_map/while
  145.0 2.2 copy-start.1
  151.8 3.1 %copy-start.2 = (f32[8,2,14336]{2,0,1:T(8,128)S(1)}, f32[8,2,14336]{2,0,1:T(8,128)}, u32[]{:S(2)}) copy-start(f32[8,2,14336]{2,0,1:T(8,128)} %copy-done.1) | copy-start | bytes 2752516 | tf_op jit(solution)/shard_map/while
Sparse Core Ops, SparseCore 0:
  156.9 62.3 all-gather.1
where the time goes:
time: 231 us; the launch traced here: 230 us
  waiting for transfers between devices  85.1 us (37%)
  matrix products  42 us (18%)
  other arithmetic  34.4 us (15%)
  local copies, waits for them, and re-layouts  25.4 us (11%)
  blocking collectives  23.1 us (10%)
  between operations  15.5 us (7%)
  starting transfers between devices  4.27 us (2%)
    all_gather x1, waiting for transfers between devices, per_device(): gathered = lax.all_gather(updated[None], 'fs', axis=1, tiled=True)  62.5 us
    dot_general x8, matrix products, learned_step(): jnp.einsum('fh,fab->hab', in_weight, features, precision=lax.Precision.HI...  25.6 us
    psum x1, blocking collectives, per_device(): lax.psum((jnp.sum(gradient * gradient), jnp.sum(mom_next * mom_next)), 'fs')  23.1 us
    all_to_all x1, waiting for transfers between devices, per_device(): lax.all_to_all(outgoing, 'ep', split_axis=1, concat_axis=0, tiled=True)  22.5 us
    mul x8, other arithmetic, learned_step(): gradient * inv_root  17.3 us
    dot_general x8, matrix products, learned_step(): jnp.einsum('hk,hab->kab', out_weight, hidden, precision=lax.Precision.HIG...  16.4 us
    another operation x8, local copies, waits for them, and re-layouts, learned_step(): jnp.stack([gradient / grad_norm, mom_next / mom_norm, mom_next * inv_root...  8.98 us
    add x2, other arithmetic, per_device(): SECOND_DECAY * second_here + (1.0 - SECOND_DECAY) * gradient * gradient  7.04 us
  transfers between devices with their start and end apart: 2, of which 2 were waited for; matrix products, arithmetic and copies ran while one was open for 0% of the time, Pallas kernels for 0%

commit v1 on v0

--- a/solution.py
+++ b/solution.py
@@ -9,6 +9,18 @@
 ROOT_EPS = 1e-08
 STEP_SCALE = 0.2
 EXP_SCALE = 0.5
+
+
+def gather_by_bits(shard, axis, dim):
+    ways, here = (lax.axis_size(axis), lax.axis_index(axis))
+    grown, reach = (shard, 1)
+    while reach < ways:
+        theirs = lax.ppermute(grown, axis, [(d, d ^ reach) for d in range(ways)])
+        mine_first = jnp.concatenate([grown, theirs], axis=dim)
+        theirs_first = jnp.concatenate([theirs, grown], axis=dim)
+        grown = jnp.where(here & reach == 0, mine_first, theirs_first)
+        reach = 2 * reach
+    return grown
 
 
 def learned_step(
@@ -95,7 +107,7 @@
         ),
     )
     updated = blocks.reshape(gradient.shape)
-    gathered = lax.all_gather(updated[None], "fs", axis=1, tiled=True)
+    gathered = gather_by_bits(updated[None], "fs", 1)
     return (gathered, mom_next[None], second_next[None])
 
 

time: 231 us -> 259 us (1.12)
  waiting for transfers between devices: 85.1 us -> 123 us
  between operations: 15.5 us -> 2.22 us
  other arithmetic: 34.4 us -> 40.3 us
  local copies, waits for them, and re-layouts: 25.4 us -> 22.1 us
    ppermute x0 -> x3, waiting for transfers between devices: none -> 101 us  [gather_by_bits(): theirs = lax.ppermute(grown, axis, [(d, d ^ reach) for d in range(ways)])]
    all_gather x1 -> x0, waiting for transfers between devices: 62.5 us -> none  [per_device(): gathered = lax.all_gather(updated[None], 'fs', axis=1, tiled=True)]
    dynamic_slice x8, local copies, waits for them, and re-layouts: 0.4 us -> 6.93 us  [per_device(): lax.map(block_step, (gradient.reshape(-1, 2, width), mom_next.reshape(-1,...]
    select_n x0 -> x4, other arithmetic: none -> 5.62 us  [gather_by_bits(): grown = jnp.where(here & reach == 0, mine_first, theirs_first)]
    dynamic_update_slice x8, local copies, waits for them, and re-layouts: 5.49 us -> 0.62 us  [per_device(): lax.map(block_step, (gradient.reshape(-1, 2, width), mom_next.reshape(-1,...]
    unnamed x13 -> x12, local copies, waits for them, and re-layouts: 4.22 us -> 0.02 us
  transfers between devices with their start and end apart: 2 -> 4, of which waited for: 2 -> 4; matrix products, arithmetic and copies ran while one was open for 0% -> 1% of each run, Pallas kernels for 0% -> 0%
where the time goes in v1:
time: 259 us; the launch traced here: 258 us
  waiting for transfers between devices  123 us (47%)
  matrix products  42 us (16%)
  other arithmetic  40.3 us (16%)
  blocking collectives  23.1 us (9%)
  local copies, waits for them, and re-layouts  22.1 us (9%)
  starting transfers between devices  4.41 us (2%)
    ppermute x3, waiting for transfers between devices, gather_by_bits(): theirs = lax.ppermute(grown, axis, [(d, d ^ reach) for d in range(ways)])  101 us
    dot_general x8, matrix products, learned_step(): jnp.einsum('fh,fab->hab', in_weight, features, precision=lax.Precision.HI...  25.6 us
    psum x1, blocking collectives, per_device(): lax.psum((jnp.sum(gradient * gradient), jnp.sum(mom_next * mom_next)), 'fs')  23.1 us
    all_to_all x1, waiting for transfers between devices, per_device(): lax.all_to_all(outgoing, 'ep', split_axis=1, concat_axis=0, tiled=True)  21.8 us
    mul x8, other arithmetic, learned_step(): gradient * inv_root  17.4 us
    dot_general x8, matrix products, learned_step(): jnp.einsum('hk,hab->kab', out_weight, hidden, precision=lax.Precision.HIG...  16.4 us
    another operation x8, local copies, waits for them, and re-layouts, learned_step(): jnp.stack([gradient / grad_norm, mom_next / mom_norm, mom_next * inv_root...  8.98 us
    add x2, other arithmetic, per_device(): SECOND_DECAY * second_here + (1.0 - SECOND_DECAY) * gradient * gradient  7.04 us
  transfers between devices with their start and end apart: 4, of which 4 were waited for; matrix products, arithmetic and copies ran while one was open for 1% of the time, Pallas kernels for 0%

profile of v1, /device:TPU:0, one launch (start us, length us, event | category | flops | bytes accessed | tf_op | source)
XLA Modules:
  0.0 257.6 jit_solution(111634860547315002)
XLA Ops:
  2.0 3.1 %multiply_convert_fusion = bf16[1,4,16,14336]{3,2,0,1:T(8,128)(2,1)} fusion(bf16[1,4,16,14336]{3,2,1,0:T(8,128)(2,1)} %param.11, f32[4]{0:T(128)S(1)} %bitcast_divide_fusion), kind=kLoop, calls=%fused_computation.23 | loop fusion | flops 2752512 | bytes 3670032 | tf_op jit(solution)/shard_map/convert_element_type | solution.py:71
  5.2 4.3 %all-to-all-start = ((bf16[1,4,16,14336]{3,2,0,1:T(8,128)(2,1)}), bf16[1,4,16,14336]{3,2,0,1:T(8,128)(2,1)S(1)}, u32[]{:S(2)}, u32[]{:S(2)}) async-start(bf16[1,4,16,14336]{3,2,0,1:T(8,128)(2,1)} %multiply_convert_fusion), calls=%async_computation | async-start | bytes 3670016 | tf_op jit(solution)/shard_map/all_to_all | solution.py:72
  10.6 21.8 %all-to-all-done = bf16[1,4,16,14336]{3,2,0,1:T(8,128)(2,1)S(1)} async-done(((bf16[1,4,16,14336]{3,2,0,1:T(8,128)(2,1)}), bf16[1,4,16,14336]{3,2,0,1:T(8,128)(2,1)S(1)}, u32[]{:S(2)}, u32[]{:S(2)}) %all-to-all-start) | async-done | bytes 1835040 | tf_op jit(solution)/shard_map/all_to_all | solution.py:72
  36.1 23.1 %all-reduce = (f32[]{:T(128)}, f32[]{:T(128)}) all-reduce(f32[]{:T(128)} %get-tuple-element.159, f32[]{:T(128)} %get-tuple-element.158), channel_id=1, replica_groups=mesh['ep'=4,'fs'=8] {'fs'}, use_global_device_ids=true, to_apply=%region_3.4 | all-reduce | flops 2 | bytes 16 | tf_op jit(solution)/shard_map/psum | solution.py:80
  59.9 3.0 %fusion.11 = (f32[1,16,14336]{2,1,0:T(8,128)}, f32[1,16,14336]{2,1,0:T(8,128)S(1)}, f32[1,16,14336]{2,1,0:T(8,128)}, f32[1,16,14336]{2,1,0:T(8,128)S(1)}) fusion(f32[16,14336]{1,0:T(8,128)S(1)} %convert_reduce_fusion, f32[1,16,14336]{2,1,0:T(8,128)} %param.15, f32[1,16,14336]{2,1,0:T(8,128)} %param.14), kind=kLoop, calls=%fused_computation.30 | loop fusion | flops 1605632 | bytes 6422528 | tf_op jit(solution)/shard_map/add | solution.py:78
  65.7 4.1 %fusion.10 = (f32[8,2,14336]{2,0,1:T(8,128)S(1)}, f32[8,2,14336]{2,0,1:T(8,128)}, f32[8,2,14336]{2,0,1:T(8,128)}) fusion(f32[8,2,14336]{2,1,0:T(2,128)S(1)} %mul.131, f32[8,2,14336]{2,1,0:T(2,128)S(1)} %copy-done, f32[8,2,14336]{2,1,0:T(2,128)} %mul.122), kind=kLoop, calls=%fused_computation.29 | loop fusion | flops 1146880 | bytes 5505024 | tf_op jit(solution)/shard_map/add | solution.py:78
  69.8 80.4 %while.11 = (s32[]{:T(128)}, bf16[8,2,14336]{2,1,0:T(2,128)(2,1)S(1)}, bf16[8,2,14336]{2,1,0:T(2,128)(2,1)}, f32[8,2,14336]{2,0,1:T(8,128)}, f32[]{:T(128)}, /*i...) while((s32[]{:T(128)}, ...), condition=%wide.region_7.8_spmd, body=%wide.region_6.7_spmd.sunk | while | flops 90316800 | bytes 18695516 | solution.py:100
  74.2 3.2 %fusion.28 = f32[32,2,14336]{2,0,1:T(8,128)S(1)} fusion(f32[6,2,14336]{2,0,1:T(8,128)S(1)} %stack.4, f32[32]{0:T(128)S(1)} %get-tuple-element.324, f32[6,32]{1,0:T(8,128)S(1)} %get-tuple-element.323), kind=kOutput, calls=%fused_computation.2.clone.1 | convolution fusion | flops 67895296 | bytes 4359040 | tf_op jit(solution)/shard_map/while/body/eval_jaxpr/fh,fab->hab/dot_general | solution.py:50
  79.8 2.2 dynamic-slice_multiply_fusion.3
  84.2 3.2 %fusion.28 = f32[32,2,14336]{2,0,1:T(8,128)S(1)} fusion(f32[6,2,14336]{2,0,1:T(8,128)S(1)} %stack.4, f32[32]{0:T(128)S(1)} %get-tuple-element.324, f32[6,32]{1,0:T(8,128)S(1)} %get-tuple-element.323), kind=kOutput, calls=%fused_computation.2.clone.1 | convolution fusion | flops 67895296 | bytes 4359040 | tf_op jit(solution)/shard_map/while/body/eval_jaxpr/fh,fab->hab/dot_general | solution.py:50
  89.9 2.2 dynamic-slice_multiply_fusion.3
  94.2 3.2 %fusion.28 = f32[32,2,14336]{2,0,1:T(8,128)S(1)} fusion(f32[6,2,14336]{2,0,1:T(8,128)S(1)} %stack.4, f32[32]{0:T(128)S(1)} %get-tuple-element.324, f32[6,32]{1,0:T(8,128)S(1)} %get-tuple-element.323), kind=kOutput, calls=%fused_computation.2.clone.1 | convolution fusion | flops 67895296 | bytes 4359040 | tf_op jit(solution)/shard_map/while/body/eval_jaxpr/fh,fab->hab/dot_general | solution.py:50
  99.9 2.2 dynamic-slice_multiply_fusion.3
  104.3 3.2 %fusion.28 = f32[32,2,14336]{2,0,1:T(8,128)S(1)} fusion(f32[6,2,14336]{2,0,1:T(8,128)S(1)} %stack.4, f32[32]{0:T(128)S(1)} %get-tuple-element.324, f32[6,32]{1,0:T(8,128)S(1)} %get-tuple-element.323), kind=kOutput, calls=%fused_computation.2.clone.1 | convolution fusion | flops 67895296 | bytes 4359040 | tf_op jit(solution)/shard_map/while/body/eval_jaxpr/fh,fab->hab/dot_general | solution.py:50
  110.0 2.2 dynamic-slice_multiply_fusion.3
  114.3 3.2 %fusion.28 = f32[32,2,14336]{2,0,1:T(8,128)S(1)} fusion(f32[6,2,14336]{2,0,1:T(8,128)S(1)} %stack.4, f32[32]{0:T(128)S(1)} %get-tuple-element.324, f32[6,32]{1,0:T(8,128)S(1)} %get-tuple-element.323), kind=kOutput, calls=%fused_computation.2.clone.1 | convolution fusion | flops 67895296 | bytes 4359040 | tf_op jit(solution)/shard_map/while/body/eval_jaxpr/fh,fab->hab/dot_general | solution.py:50
  120.0 2.2 dynamic-slice_multiply_fusion.3
  124.4 3.2 %fusion.28 = f32[32,2,14336]{2,0,1:T(8,128)S(1)} fusion(f32[6,2,14336]{2,0,1:T(8,128)S(1)} %stack.4, f32[32]{0:T(128)S(1)} %get-tuple-element.324, f32[6,32]{1,0:T(8,128)S(1)} %get-tuple-element.323), kind=kOutput, calls=%fused_computation.2.clone.1 | convolution fusion | flops 67895296 | bytes 4359040 | tf_op jit(solution)/shard_map/while/body/eval_jaxpr/fh,fab->hab/dot_general | solution.py:50
  134.4 3.2 %fusion.28 = f32[32,2,14336]{2,0,1:T(8,128)S(1)} fusion(f32[6,2,14336]{2,0,1:T(8,128)S(1)} %stack.4, f32[32]{0:T(128)S(1)} %get-tuple-element.324, f32[6,32]{1,0:T(8,128)S(1)} %get-tuple-element.323), kind=kOutput, calls=%fused_computation.2.clone.1 | convolution fusion | flops 67895296 | bytes 4359040 | tf_op jit(solution)/shard_map/while/body/eval_jaxpr/fh,fab->hab/dot_general | solution.py:50
  144.5 3.2 %fusion.28 = f32[32,2,14336]{2,0,1:T(8,128)S(1)} fusion(f32[6,2,14336]{2,0,1:T(8,128)S(1)} %stack.4, f32[32]{0:T(128)S(1)} %get-tuple-element.324, f32[6,32]{1,0:T(8,128)S(1)} %get-tuple-element.323), kind=kOutput, calls=%fused_computation.2.clone.1 | convolution fusion | flops 67895296 | bytes 4359040 | tf_op jit(solution)/shard_map/while/body/eval_jaxpr/fh,fab->hab/dot_general | solution.py:50
  150.6 8.3 %collective-permute-done = bf16[1,16,14336]{2,1,0:T(8,128)(2,1)S(1)} collective-permute-done((bf16[1,16,14336]{2,1,0:T(8,128)(2,1)S(1)}, bf16[1,16,14336]{2,1,0:T(8,128)(2,1)S(1)}, u32[]{:S(2)}, u32[]{:S(2)}) %collective-permute-start) | collective-permute-done | bytes 458784 | tf_op jit(solution)/shard_map/ppermute | solution.py:18
  159.3 16.8 %collective-permute-done.1 = bf16[1,32,14336]{2,1,0:T(8,128)(2,1)S(1)} collective-permute-done((bf16[1,32,14336]{2,1,0:T(8,128)(2,1)S(1)}, bf16[1,32,14336]{2,1,0:T(8,128)(2,1)S(1)}, u32[]{:S(2)}, u32[]{:S(2)}) %collective-permute-start.1) | collective-permute-done | bytes 917536 | tf_op jit(solution)/shard_map/ppermute | solution.py:18
  178.0 75.8 %collective-permute-done.2 = bf16[1,64,14336]{2,1,0:T(8,128)(2,1)} collective-permute-done((bf16[1,64,14336]{2,1,0:T(8,128)(2,1)}, bf16[1,64,14336]{2,1,0:T(8,128)(2,1)}, u32[]{:S(2)}, u32[]{:S(2)}) %collective-permute-start.2) | collective-permute-done | bytes 1835040 | tf_op jit(solution)/shard_map/ppermute | solution.py:18
  253.8 3.8 %maximum_select_fusion = bf16[1,128,14336]{2,1,0:T(8,128)(2,1)} fusion(bf16[1,64,14336]{2,1,0:T(8,128)(2,1)} %collective-permute-done.2, bf16[1,64,14336]{2,1,0:T(8,128)(2,1)S(1)} %fusion.9, pred[]{:T(512)S(6)} %eq.9), kind=kLoop, calls=%fused_computation.21 | loop fusion | flops 16515072 | bytes 7340033 | tf_op jit(solution)/shard_map/jit(_where)/select_n | solution.py:21
  (122 shorter events, 54.2 us)
Async XLA Ops:
  2.0 7.4 %copy-start.3 = (bf16[1,16,14336]{2,1,0:T(8,128)(2,1)S(1)}, bf16[1,16,14336]{2,1,0:T(8,128)(2,1)}, u32[]{:S(2)}) copy-start(bf16[1,16,14336]{2,1,0:T(8,128)(2,1)} %param.13) | copy-start | bytes 1376260
  5.2 27.1 %all-to-all-start = ((bf16[1,4,16,14336]{3,2,0,1:T(8,128)(2,1)}), bf16[1,4,16,14336]{3,2,0,1:T(8,128)(2,1)S(1)}, u32[]{:S(2)}, u32[]{:S(2)}) async-start(bf16[1,4,16,14336]{3,2,0,1:T(8,128)(2,1)} %multiply_convert_fusion), calls=%async_computation | async-start | bytes 3670016 | tf_op jit(solution)/shard_map/all_to_all | solution.py:72
  62.9 2.8 %copy-start = (f32[8,2,14336]{2,1,0:T(2,128)S(1)}, f32[8,2,14336]{2,1,0:T(2,128)}, u32[]{:S(2)}) copy-start(f32[8,2,14336]{2,1,0:T(2,128)} %reshape_squeeze.7) | copy-start | bytes 2752516
  64.4 5.4 %copy-start.4 = (f32[6,32]{1,0:T(8,128)S(1)}, f32[6,32]{1,0:T(8,128)}, u32[]{:S(2)}) copy-start(f32[6,32]{1,0:T(8,128)} %param.16) | copy-start | bytes 2308
  64.4 5.4 %copy-start.5 = (f32[32,2]{0,1:T(2,128)S(1)}, f32[32,2]{0,1:T(2,128)}, u32[]{:S(2)}) copy-start(f32[32,2]{0,1:T(2,128)} %param.18) | copy-start | bytes 772
  64.4 5.4 %copy-start.6 = (f32[32]{0:T(128)S(1)}, f32[32]{0:T(128)}, u32[]{:S(2)}) copy-start(f32[32]{0:T(128)} %param.17) | copy-start | bytes 388
  64.4 5.4 %copy-start.7 = (f32[2]{0:T(128)S(1)}, f32[2]{0:T(128)}, u32[]{:S(2)}) copy-start(f32[2]{0:T(128)} %param.19) | copy-start | bytes 28
  69.8 2.2 copy-start.1
  77.4 2.5 copy-start.2
  79.8 2.2 copy-start.1
  87.4 2.5 copy-start.2
  89.9 2.2 copy-start.1
  97.5 2.5 copy-start.2
  99.9 2.2 copy-start.1
  107.5 2.5 copy-start.2
  110.0 2.2 copy-start.1
  117.6 2.5 copy-start.2
  120.0 2.2 copy-start.1
  127.6 2.5 copy-start.2
  137.6 2.5 copy-start.2
  147.7 2.5 copy-start.2
  150.4 8.5 %collective-permute-start = (bf16[1,16,14336]{2,1,0:T(8,128)(2,1)S(1)}, bf16[1,16,14336]{2,1,0:T(8,128)(2,1)S(1)}, u32[]{:S(2)}, u32[]{:S(2)}) collective-permute-start(bf16[1,16,14336]{2,1,0:T(8,128)(2,1)S(1)} %broadcast_in_dim_reshape.3), channel_id=1, source_target_pairs={{0,1},{1,0},{2,3},{3,2},{4,5},{5,4},{6,7},{7,6},{8,9},{9,8},{10,11... | collective-permute-start | bytes 1376264 | tf_op jit(solution)/shard_map/ppermute | solution.py:18
  159.1 17.1 %collective-permute-start.1 = (bf16[1,32,14336]{2,1,0:T(8,128)(2,1)S(1)}, bf16[1,32,14336]{2,1,0:T(8,128)(2,1)S(1)}, u32[]{:S(2)}, u32[]{:S(2)}) collective-permute-start(bf16[1,32,14336]{2,1,0:T(8,128)(2,1)S(1)} %maximum_select_fusion.4), channel_id=1, source_target_pairs={{0,2},{1,3},{2,0},{3,1},{4,6},{5,7},{6,4},{7,5},{8,10},{9,11},{10,... | collective-permute-start | bytes 2752520 | tf_op jit(solution)/shard_map/ppermute | solution.py:18
  177.7 76.1 %collective-permute-start.2 = (bf16[1,64,14336]{2,1,0:T(8,128)(2,1)}, bf16[1,64,14336]{2,1,0:T(8,128)(2,1)}, u32[]{:S(2)}, u32[]{:S(2)}) collective-permute-start(bf16[1,64,14336]{2,1,0:T(8,128)(2,1)} %maximum_select_fusion.2), channel_id=1, source_target_pairs={{0,4},{1,5},{2,6},{3,7},{4,0},{5,1},{6,2},{7,3},{8,12},{9,13},{10,... | collective-permute-start | bytes 5505032 | tf_op jit(solution)/shard_map/ppermute | solution.py:18
  (2 other events, 4.4 us)
